TPU v7x, 256 devices: a whole 4x4x8 slice. The times are simulated.
256 devices in a mesh: ctx: 32 (over y, z), chan: 8 (over x, core).
Axes of the slice: x: 4, y: 4, z: 8, core: 2. Of those that a mesh axis runs over, the one named last changes fastest.
Arguments:
- signal: bfloat16 [128, 262144], P('chan', 'ctx'), may hold values from -6 to 6
- filter_taps: bfloat16 [8, 262144], P('chan', 'ctx'), may hold values from -1 to 1
- gate_values: bfloat16 [128, 262144], P('chan', 'ctx'), may hold values from -6 to 6
- skip_weight: float32 [128], P('chan'), may hold values from -4 to 4
Outputs:
- gated_output: bfloat16 [128, 262144], P('chan', 'ctx')
All inputs are finite; a program needn't handle non-finite values.
Results may differ from a plain program's by a relative error of at most 0.001.
Values may be sent and summed in bfloat16 or wider, within the bound.
A program may use at most 64 MiB of HBM per device.

v0:
```python
import functools

import jax
import jax.numpy as jnp
import ml_dtypes
import numpy as np
from jax import lax
from jax.experimental import pallas as pl
from jax.experimental.pallas import tpu as pltpu
from jax.sharding import Mesh
from jax.sharding import PartitionSpec as P

F32 = jnp.float32
BF16 = jnp.bfloat16
MESH = pl.DeviceIdType.MESH
PITCH = 136
HALF_ROOT = float(np.sqrt(0.5))


def two_parts(table):
    high = table.astype(ml_dtypes.bfloat16)
    low = (table - high.astype(np.float64)).astype(ml_dtypes.bfloat16)
    return np.stack([high, low])


@functools.cache
def tables():
    left, back, turn, step = [], [], [], []
    for core in range(2):
        shift = 0.125 + 0.5 * core
        kl = np.arange(128)[:, None] + shift
        angle = 2.0 * np.pi * np.mod(kl * np.arange(256)[None, :] / 128.0, 1.0)
        forward = np.concatenate([np.cos(angle), -np.sin(angle)], 0)
        left.append(two_parts(forward))
        inverse = np.roll(forward.T, -128 * core, 0)
        back.append(two_parts(inverse))
        angle = 2.0 * np.pi * np.mod(kl * np.arange(128)[None, :] / 131072.0, 1.0)
        turn.append(np.stack([np.cos(angle), -np.sin(angle)]))
        angle = np.broadcast_to(2.0 * np.pi * kl / 1024.0, (128, 128))
        step.append(np.stack([np.cos(angle), -np.sin(angle)]))
    index = np.arange(128)
    angle = 2.0 * np.pi * np.mod(index[:, None] * index[None, :] / 128.0, 1.0)
    cos, sin = np.cos(angle), np.sin(angle)
    right = two_parts(np.block([[cos, -sin], [sin, cos]]))
    undo = two_parts(np.block([[cos, sin], [-sin, cos]]) * 2.0**-18)
    angle = 2.0 * np.pi * np.arange(8)[:, None] * index[None, :] / 1024.0
    mid = np.stack([np.cos(angle), -np.sin(angle)])
    return (
        np.stack(left),
        np.stack(back),
        np.stack(turn).astype(np.float32),
        np.stack(step).astype(np.float32),
        right,
        undo,
        mid.astype(np.float32),
    )


def times(a, b):
    return (a[0] * b[0] - a[1] * b[1], a[0] * b[1] + a[1] * b[0])


def times_conj(a, b):
    return (a[0] * b[0] + a[1] * b[1], a[1] * b[0] - a[0] * b[1])


def plus(a, b):
    return (a[0] + b[0], a[1] + b[1])


def minus(a, b):
    return (a[0] - b[0], a[1] - b[1])


def quarter(a, sign):
    return (-a[1], a[0]) if sign > 0 else (a[1], -a[0])


def dft4(z, sign):
    even, odd = plus(z[0], z[2]), plus(z[1], z[3])
    d_even, d_odd = minus(z[0], z[2]), quarter(minus(z[1], z[3]), sign)
    return [plus(even, odd), plus(d_even, d_odd), minus(even, odd), minus(d_even, d_odd)]


def dft8(z, sign):
    low = [plus(z[j], z[j + 4]) for j in range(4)]
    high = [minus(z[j], z[j + 4]) for j in range(4)]
    h1 = plus(high[1], quarter(high[1], sign))
    h3 = minus(quarter(high[3], sign), high[3])
    high = [
        high[0],
        (h1[0] * HALF_ROOT, h1[1] * HALF_ROOT),
        quarter(high[2], sign),
        (h3[0] * HALF_ROOT, h3[1] * HALF_ROOT),
    ]
    even, odd = dft4(low, sign), dft4(high, sign)
    return [even[0], odd[0], even[1], odd[1], even[2], odd[2], even[3], odd[3]]


def split(value):
    high = value.astype(BF16)
    return high, (value - high.astype(F32)).astype(BF16)


def mm(a, b):
    return jnp.dot(a, b, preferred_element_type=F32)


def make_turns(turn, step, turns):
    def body(q, carry):
        rows = pl.ds(pl.multiple_of(q * 16, 16), 16)
        now = (turn[0, rows, :], turn[1, rows, :])
        by = (step[0, rows, :], step[1, rows, :])
        for a in range(8):
            turns[0, a, rows, :] = now[0]
            turns[1, a, rows, :] = now[1]
            if a < 7:
                now = times(now, by)
        return carry

    lax.fori_loop(0, 8, body, 0)


def forward_front(data, left, turns, mid, grid_f32, c_high, c_low):
    for c in range(4):
        tile = data[:, 16 * c : 16 * c + 16, :].astype(F32)
        block = jnp.concatenate(
            [tile[:, :8, :].reshape(256, 128), tile[:, 8:, :].reshape(256, 128)], axis=1
        ).astype(BF16)
        grid_f32[:, 256 * c : 256 * c + 256] = mm(left[0], block) + mm(left[1], block)

    def body(q, carry):
        at = pl.multiple_of(q * 16, 16)
        z = []
        for a in range(8):
            cols = slice(128 * a, 128 * a + 128)
            value = (grid_f32[pl.ds(at, 16), cols], grid_f32[pl.ds(at + 128, 16), cols])
            z.append(times(value, (turns[0, a, pl.ds(at, 16), :], turns[1, a, pl.ds(at, 16), :])))
        z = dft8(z, -1)
        for ka in range(8):
            value = z[ka]
            if ka:
                value = times(value, (mid[0, ka : ka + 1, :], mid[1, ka : ka + 1, :]))
            rows = pl.ds(pl.multiple_of(at + 128 * ka, 16), 16)
            for part in range(2):
                cols = slice(128 * part, 128 * part + 128)
                c_high[rows, cols], c_low[rows, cols] = split(value[part])
        return carry

    lax.fori_loop(0, 8, body, 0)


def taps_spectrum(right, c_high, c_low, spectrum):
    for m in range(4):
        rows = slice(256 * m, 256 * m + 256)
        high, low = c_high[rows, :], c_low[rows, :]
        spectrum[rows, :] = mm(high, right[0]) + mm(low, right[0]) + mm(high, right[1])


def middle(right, undo, c_high, c_low, spectrum, back_grid):
    for m in range(4):
        rows = slice(256 * m, 256 * m + 256)
        high, low = c_high[rows, :], c_low[rows, :]
        value = mm(high, right[0]) + mm(low, right[0]) + mm(high, right[1])
        taps = spectrum[rows, :]
        re, im = times((value[:, :128], value[:, 128:]), (taps[:, :128], taps[:, 128:]))
        high, low = split(jnp.concatenate([re, im], axis=1))
        back_grid[rows, :] = mm(high, undo[0]) + mm(low, undo[0]) + mm(high, undo[1])


def inverse_back(turns, mid, back_grid, d_high, d_low):
    def body(q, carry):
        at = pl.multiple_of(q * 16, 16)
        z = []
        for ka in range(8):
            rows = pl.ds(pl.multiple_of(at + 128 * ka, 16), 16)
            value = (back_grid[rows, 0:128], back_grid[rows, 128:256])
            if ka:
                value = times_conj(value, (mid[0, ka : ka + 1, :], mid[1, ka : ka + 1, :]))
            z.append(value)
        z = dft8(z, 1)
        for a in range(8):
            value = times_conj(z[a], (turns[0, a, pl.ds(at, 16), :], turns[1, a, pl.ds(at, 16), :]))
            cols = slice(128 * a, 128 * a + 128)
            for part in range(2):
                rows = pl.ds(pl.multiple_of(at + 128 * part, 16), 16)
                d_high[rows, cols], d_low[rows, cols] = split(value[part])
        return carry

    lax.fori_loop(0, 8, body, 0)


def inverse_columns(c, back, d_high, d_low):
    cols = slice(256 * c, 256 * c + 256)
    high, low = d_high[:, cols], d_low[:, cols]
    return mm(back[0], high) + mm(back[0], low) + mm(back[1], high)


def spread_out(rows_ref, work, send):
    for j in range(64):
        at = (j // 8) * PITCH + (j % 8) * 16
        work[at : at + 16, :] = rows_ref[:, 128 * j : 128 * j + 128].astype(F32)
    for r in range(16):
        for a in range(0, 8, 2):
            pair = [work[pl.ds((a + o) * 16 + r, 8, stride=PITCH), :] for o in range(2)]
            send[r, 8 * a : 8 * a + 16, :] = jnp.concatenate(pair, axis=0).astype(BF16)


def put_back(received, work, out_ref):
    for r in range(16):
        for a in range(0, 8, 2):
            pair = received[r, 8 * a : 8 * a + 16, :].astype(F32)
            for o in range(2):
                work[pl.ds((a + o) * 16 + r, 8, stride=PITCH), :] = pair[8 * o : 8 * o + 8, :]
    for j in range(64):
        at = (j // 8) * PITCH + (j % 8) * 16
        out_ref[:, 128 * j : 128 * j + 128] = work[at : at + 16, :].astype(BF16)


def kernel(
    signal, taps, gate, skip, left_all, back_all, turn_all, step_all, right_all, undo_all, mid_all, out,
    left, back, turn, step, right, undo, mid,
    work, taps_work, send_x, send_g, send_t, recv_x, recv_t, recv_g, send_o, recv_o, skips,
    turns, grid_f32, c_high, c_low, spectrum, back_grid, d_high, d_low, y_mine, y_send, y_recv,
    table_sems, sx, rx, st, rt, sg, rg, so, ro, fsx, frx, fst, frt, sy, ry, skip_sems,
):
    shard = lax.axis_index("ctx")
    core = lax.axis_index("core")
    half = lax.div(shard, 16)
    spot = lax.rem(shard, 16)
    first = 16 * core
    other = 16 - first
    mate = {"core": 1 - core}

    copies = []
    for i, (src, dst) in enumerate(
        [
            (left_all.at[core], left),
            (back_all.at[core], back),
            (turn_all.at[core], turn),
            (step_all.at[core], step),
            (right_all, right),
            (undo_all, undo),
            (mid_all, mid),
        ]
    ):
        copies.append(pltpu.make_async_copy(src, dst, table_sems.at[i]))
        copies[-1].start()

    barrier = pltpu.get_barrier_semaphore()

    def greet(i, carry):
        @pl.when(first + i != shard)
        def _():
            pl.semaphore_signal(
                barrier, inc=1, device_id={"ctx": first + i, "core": half}, device_id_type=MESH
            )

        return carry

    lax.fori_loop(0, 16, greet, 0)
    pl.semaphore_signal(barrier, inc=1, device_id=mate, device_id_type=MESH)

    for j in range(64):
        row = (j % 8) * 8 + j // 8
        taps_work[row : row + 1, :] = taps[:, 128 * j : 128 * j + 128].astype(F32)
    send_t[...] = taps_work[...].astype(BF16)
    spread_out(signal, work, send_x)
    spread_out(gate, work, send_g)
    for r in range(16):
        skips[core, r : r + 1, :] = jnp.full((1, 128), skip[r], F32)

    pl.semaphore_wait(barrier, jnp.where(core == half, 16, 17))

    def peer_copy(i, src, dst, send_sem, recv_sem):
        return pltpu.make_async_remote_copy(
            src_ref=src,
            dst_ref=dst,
            send_sem=send_sem.at[i],
            recv_sem=recv_sem,
            device_id={"ctx": first + i, "core": half},
            device_id_type=MESH,
        )

    def each_peer(remote, here=None):
        def body(k, carry):
            i = lax.rem(spot + k, 16)

            @pl.when(first + i != shard)
            def _():
                remote(i)

            if here is not None:

                @pl.when(first + i == shard)
                def _():
                    here(i)

            return carry

        lax.fori_loop(0, 16, body, 0)

    def out_t(i):
        return peer_copy(i, send_t, recv_t.at[shard], st, rt.at[spot])

    def out_x(i):
        return peer_copy(i, send_x.at[i], recv_x.at[shard], sx, rx.at[spot])

    def out_g(i):
        return peer_copy(i, send_g.at[i], recv_g.at[spot], sg, rg.at[spot])

    def out_o(i):
        return peer_copy(i, send_o.at[i], recv_o.at[spot], so, ro.at[spot])

    def keep_t(i):
        recv_t[shard] = send_t[...]

    def keep_x(i):
        recv_x[shard] = send_x[i]

    def keep_g(i):
        recv_g[spot] = send_g[i]

    skip_copy = pltpu.make_async_remote_copy(
        src_ref=skips.at[core], dst_ref=skips.at[core], send_sem=skip_sems.at[0],
        recv_sem=skip_sems.at[1], device_id=mate, device_id_type=MESH,
    )
    each_peer(lambda i: out_t(i).start(), keep_t)
    each_peer(lambda i: out_x(i).start(), keep_x)
    each_peer(lambda i: out_g(i).start(), keep_g)
    skip_copy.start()

    def incoming(i, src, slot, recv_sem):
        return pltpu.make_async_remote_copy(
            src_ref=src, dst_ref=slot, send_sem=st.at[i], recv_sem=recv_sem.at[i],
            device_id={"ctx": first + i, "core": half}, device_id_type=MESH,
        )

    def to_mate(i, ref, slot, send_sem, recv_sem):
        return pltpu.make_async_remote_copy(
            src_ref=ref.at[slot], dst_ref=ref.at[slot], send_sem=send_sem.at[i],
            recv_sem=recv_sem.at[i], device_id=mate, device_id_type=MESH,
        )

    def gather(ref, recv_sem, fwd_send, fwd_recv):
        def pass_on(k, carry):
            i = lax.rem(spot + k, 16)

            @pl.when(first + i != shard)
            def _():
                incoming(i, send_t, ref.at[first + i], recv_sem).wait_recv()

            to_mate(i, ref, first + i, fwd_send, fwd_recv).start()
            return carry

        lax.fori_loop(0, 16, pass_on, 0)

        def take(i, carry):
            to_mate(i, ref, other + i, fwd_send, fwd_recv).wait_recv()
            return carry

        lax.fori_loop(0, 16, take, 0)

    for copy in copies:
        copy.wait()
    make_turns(turn, step, turns)

    gather(recv_t, rt, fst, frt)
    forward_front(recv_t, left, turns, mid, grid_f32, c_high, c_low)
    taps_spectrum(right, c_high, c_low, spectrum)
    gather(recv_x, rx, fsx, frx)
    forward_front(recv_x, left, turns, mid, grid_f32, c_high, c_low)
    middle(right, undo, c_high, c_low, spectrum, back_grid)
    inverse_back(turns, mid, back_grid, d_high, d_low)

    def y_copy(c):
        return pltpu.make_async_remote_copy(
            src_ref=y_send.at[c], dst_ref=y_recv.at[c], send_sem=sy.at[c], recv_sem=ry.at[c],
            device_id=mate, device_id_type=MESH,
        )

    for c in range(4):
        value = inverse_columns(c, back, d_high, d_low)
        y_send[c] = value[128:, :]
        y_mine[c] = value[:128, :]
        y_copy(c).start()
    skip_copy.wait()
    weight = skips[half, pl.ds(spot, 1), :]
    each_peer(lambda i: incoming(i, send_t, recv_g.at[i], rg).wait_recv())
    for c in range(4):
        y_copy(c).wait_recv()

    def finish(i):
        rows = pl.ds(pl.multiple_of(i * 8, 8), 8)
        for c in range(4):
            total = y_mine[c, rows, :] + y_recv[c, rows, :]
            total = jnp.concatenate([total[:, :128], total[:, 128:]], axis=0)
            cut = slice(16 * c, 16 * c + 16)
            direct = recv_x[first + i, cut, :].astype(F32)
            total = recv_g[i, cut, :].astype(F32) * (total + weight * direct)
            send_o[i, cut, :] = total.astype(BF16)

    def send_back(i):
        finish(i)
        out_o(i).start()

    def keep_o(i):
        finish(i)
        recv_o[spot] = send_o[i]

    each_peer(send_back, keep_o)
    each_peer(lambda i: incoming(i, send_t, recv_o.at[i], ro).wait_recv())
    put_back(recv_o, work, out)

    def sent(i):
        out_t(i).wait_send()
        out_x(i).wait_send()
        out_g(i).wait_send()
        out_o(i).wait_send()

    each_peer(sent)

    def passed(i, carry):
        to_mate(i, recv_t, first + i, fst, frt).wait_send()
        to_mate(i, recv_x, first + i, fsx, frx).wait_send()
        return carry

    lax.fori_loop(0, 16, passed, 0)
    for c in range(4):
        y_copy(c).wait_send()


def local(signal, filter_taps, gate_values, skip_weight):
    held = tables()
    vmem, dma = pltpu.VMEM, pltpu.SemaphoreType.DMA
    whole = pl.BlockSpec(memory_space=pltpu.VMEM)
    apart = pl.BlockSpec(memory_space=pl.ANY)
    scratch = [
        vmem((2, 256, 256), BF16),
        vmem((2, 256, 256), BF16),
        vmem((2, 128, 128), F32),
        vmem((2, 128, 128), F32),
        vmem((2, 256, 256), BF16),
        vmem((2, 256, 256), BF16),
        vmem((2, 8, 128), F32),
        vmem((8 * PITCH, 128), F32),
        vmem((64, 128), F32),
        vmem((16, 64, 128), BF16),
        vmem((16, 64, 128), BF16),
        vmem((64, 128), BF16),
        vmem((32, 64, 128), BF16),
        vmem((32, 64, 128), BF16),
        vmem((16, 64, 128), BF16),
        vmem((16, 64, 128), BF16),
        vmem((16, 64, 128), BF16),
        vmem((2, 16, 128), F32),
        vmem((2, 8, 128, 128), F32),
        vmem((256, 1024), F32),
        vmem((1024, 256), BF16),
        vmem((1024, 256), BF16),
        vmem((1024, 256), F32),
        vmem((1024, 256), F32),
        vmem((256, 1024), BF16),
        vmem((256, 1024), BF16),
        vmem((4, 128, 256), F32),
        vmem((4, 128, 256), F32),
        vmem((4, 128, 256), F32),
        dma((7,)),
        *[dma((16,)) for _ in range(12)],
        dma((4,)),
        dma((4,)),
        dma((2,)),
    ]
    return pl.pallas_call(
        kernel,
        out_shape=jax.ShapeDtypeStruct(signal.shape, BF16),
        in_specs=[whole, whole, whole, pl.BlockSpec(memory_space=pltpu.SMEM)] + [apart] * len(held),
        out_specs=whole,
        scratch_shapes=scratch,
        compiler_params=pltpu.CompilerParams(collective_id=0, has_side_effects=True),
        name="hyena",
    )(signal, filter_taps, gate_values, skip_weight, *[jnp.asarray(t) for t in held])


def solution(mesh):
    shards = mesh.shape["ctx"]
    finer = Mesh(mesh.devices.reshape(shards, -1, 2), ("ctx", "x", "core"))
    chan = ("x", "core")
    placed = (P(chan, "ctx"), P(chan, "ctx"), P(chan, "ctx"), P(chan))
    return jax.shard_map(
        local, mesh=finer, in_specs=placed, out_specs=P(chan, "ctx"), check_vma=False
    )
```

profile of v0, /device:TPU:1, one launch (start us, length us, event | category | flops | bytes accessed | tf_op | source)
XLA Modules:
  0.0 47.5 jit_solution(3176841917512185844)
XLA Ops:
  0.0 45.9 %hyena.1 = bf16[16,8192]{1,0:T(8,128)(2,1)} custom-call(bf16[16,8192]{1,0:T(8,128)(2,1)} %signal.1, bf16[1,8192]{1,0:T(2,128)(2,1)} %taps.1, bf16[16,8192]{1,0:T(8,128)(2,1)} %gate.1, f32[16]{0:T(128)} %skip.1, bf16[2,2,256,256]{3,2,1,0:T(8,128)(2,1)} %constant.14.clone.left_all, bf16[2,2,256,256]{3,2,1,0:T(8,128)(2,1)} %constant.15.clone.back_all, ...), custom_call_target="tpu_custom_call" | custom-call | tf_op jit(solution)/shard_map/hyena/pallas_call | solution.py:474
  45.9 1.7 %copy.13 = bf16[16,8192]{1,0:T(8,128)(2,1)} copy(bf16[16,8192]{1,0:T(8,128)(2,1)} %hyena.1) | data formatting | bytes 524288
where the time goes:
time: 47.7 us; the launch traced here: 47.5 us
  Pallas kernels  45.9 us (96%)
  local copies, waits for them, and re-layouts  1.67 us (4%)
    pallas_call x1, Pallas kernels, local(): pl.pallas_call(kernel, out_shape=jax.ShapeDtypeStruct(signal.shape, BF16)...  45.9 us
    unnamed x1, local copies, waits for them, and re-layouts  1.67 us

commit v1 on v0

--- a/solution.py
+++ b/solution.py
@@ -206,23 +206,27 @@
             send[r, 8 * a : 8 * a + 16, :] = jnp.concatenate(pair, axis=0).astype(BF16)
 
 
-def put_back(received, work, out_ref):
-    for r in range(16):
-        for a in range(0, 8, 2):
-            pair = received[r, 8 * a : 8 * a + 16, :].astype(F32)
-            for o in range(2):
-                work[pl.ds((a + o) * 16 + r, 8, stride=PITCH), :] = pair[8 * o : 8 * o + 8, :]
-    for j in range(64):
-        at = (j // 8) * PITCH + (j % 8) * 16
-        out_ref[:, 128 * j : 128 * j + 128] = work[at : at + 16, :].astype(BF16)
+def put_row(received, work, r):
+    for a in range(0, 8, 2):
+        pair = received[r, 8 * a : 8 * a + 16, :].astype(F32)
+        for o in range(2):
+            work[pl.ds((a + o) * 16 + r, 8, stride=PITCH), :] = pair[8 * o : 8 * o + 8, :]
+
+
+def start_order(ctx, core):
+    z, y = lax.rem(ctx, 8), lax.div(ctx, 8)
+    return (jnp.minimum(z, 4) * 10 + y * 6 + (1 - core) * 4) * 64 + ctx * 2 + core
 
 
 def kernel(
-    signal, taps, gate, skip, left_all, back_all, turn_all, step_all, right_all, undo_all, mid_all, out,
+    signal_in, taps_in, gate_in, skip_in, left_all, back_all, turn_all, step_all, right_all, undo_all, mid_all,
+    out_all,
+    signal, taps, gate, skip, out,
     left, back, turn, step, right, undo, mid,
     work, taps_work, send_x, send_g, send_t, recv_x, recv_t, recv_g, send_o, recv_o, skips,
     turns, grid_f32, c_high, c_low, spectrum, back_grid, d_high, d_low, y_mine, y_send, y_recv,
-    table_sems, sx, rx, st, rt, sg, rg, so, ro, fsx, frx, fst, frt, sy, ry, skip_sems,
+    input_sems, table_sems, out_sems,
+    sx, rx, st, rt, sg, rg, so, ro, fsx, frx, fst, frt, sy, ry, skip_sems, ready,
 ):
     shard = lax.axis_index("ctx")
     core = lax.axis_index("core")
@@ -231,110 +235,165 @@
     first = 16 * core
     other = 16 - first
     mate = {"core": 1 - core}
-
-    copies = []
-    for i, (src, dst) in enumerate(
+    mine = start_order(shard, core)
+    mate_later = start_order(shard, 1 - core) > mine
+
+    def peer_later(i):
+        return start_order(first + i, half) > mine
+
+    def peer_earlier(i):
+        return start_order(first + i, half) < mine
+
+    def peer(i):
+        return {"ctx": first + i, "core": half}
+
+    def all_peers(body):
+        def run(k, carry):
+            body(lax.rem(spot + k, 16))
+            return carry
+
+        lax.fori_loop(0, 16, run, 0)
+
+    barrier = pltpu.get_barrier_semaphore()
+
+    def greet(i):
+        @pl.when(peer_later(i))
+        def _():
+            pl.semaphore_signal(barrier, inc=1, device_id=peer(i), device_id_type=MESH)
+
+    all_peers(greet)
+
+    @pl.when(mate_later)
+    def _():
+        pl.semaphore_signal(barrier, inc=1, device_id=mate, device_id_type=MESH)
+
+    def fetch(pairs, sems):
+        copies = [pltpu.make_async_copy(a, b, sems.at[i]) for i, (a, b) in enumerate(pairs)]
+        for copy in copies:
+            copy.start()
+        return copies
+
+    inputs = fetch(
+        [(taps_in, taps), (signal_in, signal), (gate_in, gate), (skip_in, skip)], input_sems
+    )
+    copies = fetch(
         [
             (left_all.at[core], left),
-            (back_all.at[core], back),
             (turn_all.at[core], turn),
             (step_all.at[core], step),
             (right_all, right),
+            (mid_all, mid),
             (undo_all, undo),
-            (mid_all, mid),
-        ]
-    ):
-        copies.append(pltpu.make_async_copy(src, dst, table_sems.at[i]))
-        copies[-1].start()
-
-    barrier = pltpu.get_barrier_semaphore()
-
-    def greet(i, carry):
-        @pl.when(first + i != shard)
-        def _():
-            pl.semaphore_signal(
-                barrier, inc=1, device_id={"ctx": first + i, "core": half}, device_id_type=MESH
-            )
-
-        return carry
-
-    lax.fori_loop(0, 16, greet, 0)
-    pl.semaphore_signal(barrier, inc=1, device_id=mate, device_id_type=MESH)
-
+            (back_all.at[core], back),
+        ],
+        table_sems,
+    )
+
+    inputs[0].wait()
     for j in range(64):
         row = (j % 8) * 8 + j // 8
         taps_work[row : row + 1, :] = taps[:, 128 * j : 128 * j + 128].astype(F32)
     send_t[...] = taps_work[...].astype(BF16)
+    inputs[1].wait()
     spread_out(signal, work, send_x)
+
+    earlier = lax.fori_loop(
+        0, 16, lambda i, n: n + jnp.where(peer_earlier(i), 1, 0), jnp.where(mate_later, 0, 1)
+    )
+
+    @pl.when(earlier > 0)
+    def _():
+        pl.semaphore_wait(barrier, earlier)
+
+    def answer(i):
+        @pl.when(peer_earlier(i))
+        def _():
+            pl.semaphore_signal(ready.at[spot], inc=1, device_id=peer(i), device_id_type=MESH)
+
+    all_peers(answer)
+
+    @pl.when(jnp.logical_not(mate_later))
+    def _():
+        pl.semaphore_signal(ready.at[16], inc=1, device_id=mate, device_id_type=MESH)
+
+    def peer_copy(i, src, dst, send_sem, recv_sem):
+        return pltpu.make_async_remote_copy(
+            src_ref=src, dst_ref=dst, send_sem=send_sem.at[i], recv_sem=recv_sem,
+            device_id=peer(i), device_id_type=MESH,
+        )
+
+    def others(body):
+        def run(i):
+            @pl.when(first + i != shard)
+            def _():
+                body(i)
+
+        all_peers(run)
+
+    def out_t(i):
+        return peer_copy(i, send_t, recv_t.at[shard], st, rt.at[spot])
+
+    def out_x(i):
+        return peer_copy(i, send_x.at[i], recv_x.at[shard], sx, rx.at[spot])
+
+    def out_g(i):
+        return peer_copy(i, send_g.at[i], recv_g.at[spot], sg, rg.at[spot])
+
+    def out_o(i):
+        return peer_copy(i, send_o.at[i], recv_o.at[spot], so, ro.at[spot])
+
+    def if_earlier(body):
+        def run(i):
+            @pl.when(peer_earlier(i))
+            def _():
+                body(i)
+
+        return run
+
+    all_peers(if_earlier(lambda i: out_t(i).start()))
+    all_peers(if_earlier(lambda i: out_x(i).start()))
+
+    @pl.when(core == half)
+    def _():
+        recv_t[shard] = send_t[...]
+        recv_x[shard] = send_x[spot]
+
+    def later_in_turn(k, carry):
+        i = lax.rem(k, 2) * 8 + lax.div(k, 2)
+
+        @pl.when(peer_later(i))
+        def _():
+            pl.semaphore_wait(ready.at[i], 1)
+            out_t(i).start()
+            out_x(i).start()
+
+        return carry
+
+    lax.fori_loop(0, 16, later_in_turn, 0)
+
+    @pl.when(mate_later)
+    def _():
+        pl.semaphore_wait(ready.at[16], 1)
+
+    inputs[2].wait()
     spread_out(gate, work, send_g)
+    others(lambda i: out_g(i).start())
+
+    @pl.when(core == half)
+    def _():
+        recv_g[spot] = send_g[spot]
+
+    inputs[3].wait()
     for r in range(16):
         skips[core, r : r + 1, :] = jnp.full((1, 128), skip[r], F32)
-
-    pl.semaphore_wait(barrier, jnp.where(core == half, 16, 17))
-
-    def peer_copy(i, src, dst, send_sem, recv_sem):
-        return pltpu.make_async_remote_copy(
-            src_ref=src,
-            dst_ref=dst,
-            send_sem=send_sem.at[i],
-            recv_sem=recv_sem,
-            device_id={"ctx": first + i, "core": half},
-            device_id_type=MESH,
-        )
-
-    def each_peer(remote, here=None):
-        def body(k, carry):
-            i = lax.rem(spot + k, 16)
-
-            @pl.when(first + i != shard)
-            def _():
-                remote(i)
-
-            if here is not None:
-
-                @pl.when(first + i == shard)
-                def _():
-                    here(i)
-
-            return carry
-
-        lax.fori_loop(0, 16, body, 0)
-
-    def out_t(i):
-        return peer_copy(i, send_t, recv_t.at[shard], st, rt.at[spot])
-
-    def out_x(i):
-        return peer_copy(i, send_x.at[i], recv_x.at[shard], sx, rx.at[spot])
-
-    def out_g(i):
-        return peer_copy(i, send_g.at[i], recv_g.at[spot], sg, rg.at[spot])
-
-    def out_o(i):
-        return peer_copy(i, send_o.at[i], recv_o.at[spot], so, ro.at[spot])
-
-    def keep_t(i):
-        recv_t[shard] = send_t[...]
-
-    def keep_x(i):
-        recv_x[shard] = send_x[i]
-
-    def keep_g(i):
-        recv_g[spot] = send_g[i]
-
     skip_copy = pltpu.make_async_remote_copy(
         src_ref=skips.at[core], dst_ref=skips.at[core], send_sem=skip_sems.at[0],
         recv_sem=skip_sems.at[1], device_id=mate, device_id_type=MESH,
     )
-    each_peer(lambda i: out_t(i).start(), keep_t)
-    each_peer(lambda i: out_x(i).start(), keep_x)
-    each_peer(lambda i: out_g(i).start(), keep_g)
     skip_copy.start()
 
-    def incoming(i, src, slot, recv_sem):
-        return pltpu.make_async_remote_copy(
-            src_ref=src, dst_ref=slot, send_sem=st.at[i], recv_sem=recv_sem.at[i],
-            device_id={"ctx": first + i, "core": half}, device_id_type=MESH,
-        )
+    def incoming(i, slot, recv_sem):
+        return peer_copy(i, send_t, slot, st, recv_sem.at[i])
 
     def to_mate(i, ref, slot, send_sem, recv_sem):
         return pltpu.make_async_remote_copy(
@@ -343,17 +402,14 @@
         )
 
     def gather(ref, recv_sem, fwd_send, fwd_recv):
-        def pass_on(k, carry):
-            i = lax.rem(spot + k, 16)
-
+        def pass_on(i):
             @pl.when(first + i != shard)
             def _():
-                incoming(i, send_t, ref.at[first + i], recv_sem).wait_recv()
+                incoming(i, ref.at[first + i], recv_sem).wait_recv()
 
             to_mate(i, ref, first + i, fwd_send, fwd_recv).start()
-            return carry
-
-        lax.fori_loop(0, 16, pass_on, 0)
+
+        all_peers(pass_on)
 
         def take(i, carry):
             to_mate(i, ref, other + i, fwd_send, fwd_recv).wait_recv()
@@ -386,11 +442,11 @@
         y_copy(c).start()
     skip_copy.wait()
     weight = skips[half, pl.ds(spot, 1), :]
-    each_peer(lambda i: incoming(i, send_t, recv_g.at[i], rg).wait_recv())
+    others(lambda i: incoming(i, recv_g.at[i], rg).wait_recv())
     for c in range(4):
         y_copy(c).wait_recv()
 
-    def finish(i):
+    def send_back(i):
         rows = pl.ds(pl.multiple_of(i * 8, 8), 8)
         for c in range(4):
             total = y_mine[c, rows, :] + y_recv[c, rows, :]
@@ -400,17 +456,32 @@
             total = recv_g[i, cut, :].astype(F32) * (total + weight * direct)
             send_o[i, cut, :] = total.astype(BF16)
 
-    def send_back(i):
-        finish(i)
-        out_o(i).start()
-
-    def keep_o(i):
-        finish(i)
-        recv_o[spot] = send_o[i]
-
-    each_peer(send_back, keep_o)
-    each_peer(lambda i: incoming(i, send_t, recv_o.at[i], ro).wait_recv())
-    put_back(recv_o, work, out)
+        @pl.when(first + i != shard)
+        def _():
+            out_o(i).start()
+
+        @pl.when(first + i == shard)
+        def _():
+            recv_o[spot] = send_o[i]
+
+    all_peers(send_back)
+
+    def place(i):
+        @pl.when(first + i != shard)
+        def _():
+            incoming(i, recv_o.at[i], ro).wait_recv()
+
+        put_row(recv_o, work, i)
+
+    all_peers(place)
+    results = []
+    for piece in range(4):
+        for j in range(16 * piece, 16 * piece + 16):
+            at = (j // 8) * PITCH + (j % 8) * 16
+            out[piece, :, 128 * (j % 16) : 128 * (j % 16) + 128] = work[at : at + 16, :].astype(BF16)
+        cols = slice(2048 * piece, 2048 * piece + 2048)
+        results.append(pltpu.make_async_copy(out.at[piece], out_all.at[:, cols], out_sems.at[piece]))
+        results[-1].start()
 
     def sent(i):
         out_t(i).wait_send()
@@ -418,7 +489,7 @@
         out_g(i).wait_send()
         out_o(i).wait_send()
 
-    each_peer(sent)
+    others(sent)
 
     def passed(i, carry):
         to_mate(i, recv_t, first + i, fst, frt).wait_send()
@@ -428,14 +499,20 @@
     lax.fori_loop(0, 16, passed, 0)
     for c in range(4):
         y_copy(c).wait_send()
+    for result in results:
+        result.wait()
 
 
 def local(signal, filter_taps, gate_values, skip_weight):
     held = tables()
     vmem, dma = pltpu.VMEM, pltpu.SemaphoreType.DMA
-    whole = pl.BlockSpec(memory_space=pltpu.VMEM)
     apart = pl.BlockSpec(memory_space=pl.ANY)
     scratch = [
+        vmem((16, 8192), BF16),
+        vmem((1, 8192), BF16),
+        vmem((16, 8192), BF16),
+        pltpu.SMEM((16,), F32),
+        vmem((4, 16, 2048), BF16),
         vmem((2, 256, 256), BF16),
         vmem((2, 256, 256), BF16),
         vmem((2, 128, 128), F32),
@@ -465,17 +542,20 @@
         vmem((4, 128, 256), F32),
         vmem((4, 128, 256), F32),
         vmem((4, 128, 256), F32),
+        dma((4,)),
         dma((7,)),
+        dma((4,)),
         *[dma((16,)) for _ in range(12)],
         dma((4,)),
         dma((4,)),
         dma((2,)),
+        pltpu.SemaphoreType.REGULAR((17,)),
     ]
     return pl.pallas_call(
         kernel,
         out_shape=jax.ShapeDtypeStruct(signal.shape, BF16),
-        in_specs=[whole, whole, whole, pl.BlockSpec(memory_space=pltpu.SMEM)] + [apart] * len(held),
-        out_specs=whole,
+        in_specs=[apart] * (4 + len(held)),
+        out_specs=apart,
         scratch_shapes=scratch,
         compiler_params=pltpu.CompilerParams(collective_id=0, has_side_effects=True),
         name="hyena",

time: 47.7 us -> 50.5 us (1.059)
  Pallas kernels: 45.9 us -> 48.7 us
    pallas_call x1, Pallas kernels: 45.9 us -> 48.7 us  [local(): pl.pallas_call(kernel, out_shape=jax.ShapeDtypeStruct(signal.shape, BF16)...]
where the time goes in v1:
time: 50.5 us; the launch traced here: 50.3 us
  Pallas kernels  48.7 us (96%)
  local copies, waits for them, and re-layouts  1.67 us (3%)
    pallas_call x1, Pallas kernels, local(): pl.pallas_call(kernel, out_shape=jax.ShapeDtypeStruct(signal.shape, BF16)...  48.7 us
    unnamed x1, local copies, waits for them, and re-layouts  1.67 us

profile of v1, /device:TPU:1, one launch (start us, length us, event | category | flops | bytes accessed | tf_op | source)
XLA Modules:
  0.0 50.3 jit_solution(4103226827554312012)
XLA Ops:
  0.0 48.7 %hyena.1 = bf16[16,8192]{1,0:T(8,128)(2,1)} custom-call(bf16[16,8192]{1,0:T(8,128)(2,1)} %signal_in.1, bf16[1,8192]{1,0:T(2,128)(2,1)} %taps_in.1, bf16[16,8192]{1,0:T(8,128)(2,1)} %gate_in.1, f32[16]{0:T(128)} %skip_in.1, bf16[2,2,256,256]{3,2,1,0:T(8,128)(2,1)} %constant.14.clone.left_all, bf16[2,2,256,256]{3,2,1,0:T(8,128)(2,1)} %constant.15.clone.back_all, ...), custom_call_target="tpu_custom_call" | custom-call | tf_op jit(solution)/shard_map/hyena/pallas_call | solution.py:554
  48.7 1.7 %copy.13 = bf16[16,8192]{1,0:T(8,128)(2,1)} copy(bf16[16,8192]{1,0:T(8,128)(2,1)} %hyena.1) | data formatting | bytes 524288

commit v2 on v1

--- a/solution.py
+++ b/solution.py
@@ -213,20 +213,15 @@
             work[pl.ds((a + o) * 16 + r, 8, stride=PITCH), :] = pair[8 * o : 8 * o + 8, :]
 
 
-def start_order(ctx, core):
-    z, y = lax.rem(ctx, 8), lax.div(ctx, 8)
-    return (jnp.minimum(z, 4) * 10 + y * 6 + (1 - core) * 4) * 64 + ctx * 2 + core
-
-
 def kernel(
     signal_in, taps_in, gate_in, skip_in, left_all, back_all, turn_all, step_all, right_all, undo_all, mid_all,
     out_all,
     signal, taps, gate, skip, out,
     left, back, turn, step, right, undo, mid,
-    work, taps_work, send_x, send_g, send_t, recv_x, recv_t, recv_g, send_o, recv_o, skips,
+    work, taps_work, send_x, send_g, send_t, ring_t, recv_x, recv_t, recv_g, send_o, recv_o, skips,
     turns, grid_f32, c_high, c_low, spectrum, back_grid, d_high, d_low, y_mine, y_send, y_recv,
     input_sems, table_sems, out_sems,
-    sx, rx, st, rt, sg, rg, so, ro, fsx, frx, fst, frt, sy, ry, skip_sems, ready,
+    sr, rr, sx, rx, st, rt, sg, rg, so, ro, fsx, frx, fst, frt, sy, ry, skip_sems,
 ):
     shard = lax.axis_index("ctx")
     core = lax.axis_index("core")
@@ -235,14 +230,8 @@
     first = 16 * core
     other = 16 - first
     mate = {"core": 1 - core}
-    mine = start_order(shard, core)
-    mate_later = start_order(shard, 1 - core) > mine
-
-    def peer_later(i):
-        return start_order(first + i, half) > mine
-
-    def peer_earlier(i):
-        return start_order(first + i, half) < mine
+    row = lax.div(shard, 8)
+    col = lax.rem(shard, 8)
 
     def peer(i):
         return {"ctx": first + i, "core": half}
@@ -256,16 +245,33 @@
 
     barrier = pltpu.get_barrier_semaphore()
 
-    def greet(i):
-        @pl.when(peer_later(i))
-        def _():
-            pl.semaphore_signal(barrier, inc=1, device_id=peer(i), device_id_type=MESH)
-
-    all_peers(greet)
-
-    @pl.when(mate_later)
+    def others(body):
+        def run(i):
+            @pl.when(first + i != shard)
+            def _():
+                body(i)
+
+        all_peers(run)
+
+    def ring(i):
+        return {"ctx": row * 8 + i}
+
+    def along_ring(body):
+        def run(k, carry):
+            body(lax.rem(col + k, 8))
+            return carry
+
+        lax.fori_loop(1, 8, run, 0)
+
+    def hello(device):
+        pl.semaphore_signal(barrier, inc=1, device_id=device, device_id_type=MESH)
+
+    others(lambda i: hello(peer(i)))
+    hello(mate)
+
+    @pl.when(core != half)
     def _():
-        pl.semaphore_signal(barrier, inc=1, device_id=mate, device_id_type=MESH)
+        along_ring(lambda i: hello(ring(i)))
 
     def fetch(pairs, sems):
         copies = [pltpu.make_async_copy(a, b, sems.at[i]) for i, (a, b) in enumerate(pairs)]
@@ -291,30 +297,13 @@
 
     inputs[0].wait()
     for j in range(64):
-        row = (j % 8) * 8 + j // 8
-        taps_work[row : row + 1, :] = taps[:, 128 * j : 128 * j + 128].astype(F32)
+        at = (j % 8) * 8 + j // 8
+        taps_work[at : at + 1, :] = taps[:, 128 * j : 128 * j + 128].astype(F32)
     send_t[...] = taps_work[...].astype(BF16)
     inputs[1].wait()
     spread_out(signal, work, send_x)
 
-    earlier = lax.fori_loop(
-        0, 16, lambda i, n: n + jnp.where(peer_earlier(i), 1, 0), jnp.where(mate_later, 0, 1)
-    )
-
-    @pl.when(earlier > 0)
-    def _():
-        pl.semaphore_wait(barrier, earlier)
-
-    def answer(i):
-        @pl.when(peer_earlier(i))
-        def _():
-            pl.semaphore_signal(ready.at[spot], inc=1, device_id=peer(i), device_id_type=MESH)
-
-    all_peers(answer)
-
-    @pl.when(jnp.logical_not(mate_later))
-    def _():
-        pl.semaphore_signal(ready.at[16], inc=1, device_id=mate, device_id_type=MESH)
+    pl.semaphore_wait(barrier, jnp.where(core == half, 16, 24))
 
     def peer_copy(i, src, dst, send_sem, recv_sem):
         return pltpu.make_async_remote_copy(
@@ -322,16 +311,18 @@
             device_id=peer(i), device_id_type=MESH,
         )
 
-    def others(body):
-        def run(i):
-            @pl.when(first + i != shard)
-            def _():
-                body(i)
-
-        all_peers(run)
-
-    def out_t(i):
-        return peer_copy(i, send_t, recv_t.at[shard], st, rt.at[spot])
+    def ring_copy(i, slot):
+        return pltpu.make_async_remote_copy(
+            src_ref=send_t, dst_ref=ring_t.at[slot], send_sem=sr.at[i], recv_sem=rr.at[slot],
+            device_id=ring(i), device_id_type=MESH,
+        )
+
+    def row_copy(block, side):
+        i = side * 8 + col
+        return pltpu.make_async_remote_copy(
+            src_ref=ring_t.at[block], dst_ref=recv_t.at[row * 8 + block], send_sem=st.at[side * 8 + block],
+            recv_sem=rt.at[lax.rem(row, 2) * 8 + block], device_id=peer(i), device_id_type=MESH,
+        )
 
     def out_x(i):
         return peer_copy(i, send_x.at[i], recv_x.at[shard], sx, rx.at[spot])
@@ -342,38 +333,13 @@
     def out_o(i):
         return peer_copy(i, send_o.at[i], recv_o.at[spot], so, ro.at[spot])
 
-    def if_earlier(body):
-        def run(i):
-            @pl.when(peer_earlier(i))
-            def _():
-                body(i)
-
-        return run
-
-    all_peers(if_earlier(lambda i: out_t(i).start()))
-    all_peers(if_earlier(lambda i: out_x(i).start()))
+    along_ring(lambda i: ring_copy(i, col).start())
+    ring_t[col] = send_t[...]
+    others(lambda i: out_x(i).start())
 
     @pl.when(core == half)
     def _():
-        recv_t[shard] = send_t[...]
         recv_x[shard] = send_x[spot]
-
-    def later_in_turn(k, carry):
-        i = lax.rem(k, 2) * 8 + lax.div(k, 2)
-
-        @pl.when(peer_later(i))
-        def _():
-            pl.semaphore_wait(ready.at[i], 1)
-            out_t(i).start()
-            out_x(i).start()
-
-        return carry
-
-    lax.fori_loop(0, 16, later_in_turn, 0)
-
-    @pl.when(mate_later)
-    def _():
-        pl.semaphore_wait(ready.at[16], 1)
 
     inputs[2].wait()
     spread_out(gate, work, send_g)
@@ -393,7 +359,26 @@
     skip_copy.start()
 
     def incoming(i, slot, recv_sem):
-        return peer_copy(i, send_t, slot, st, recv_sem.at[i])
+        return peer_copy(i, send_t, slot, sx, recv_sem.at[i])
+
+    def to_rows(block):
+        for side in range(2):
+
+            @pl.when(first + side * 8 + col != shard)
+            def _():
+                row_copy(block, side).start()
+
+        @pl.when(core == half)
+        def _():
+            recv_t[row * 8 + block] = ring_t[block]
+
+    to_rows(col)
+
+    def relay(i):
+        ring_copy(i, i).wait_recv()
+        to_rows(i)
+
+    along_ring(relay)
 
     def to_mate(i, ref, slot, send_sem, recv_sem):
         return pltpu.make_async_remote_copy(
@@ -401,9 +386,9 @@
             recv_sem=recv_sem.at[i], device_id=mate, device_id_type=MESH,
         )
 
-    def gather(ref, recv_sem, fwd_send, fwd_recv):
+    def gather(ref, recv_sem, fwd_send, fwd_recv, remote):
         def pass_on(i):
-            @pl.when(first + i != shard)
+            @pl.when(remote(i))
             def _():
                 incoming(i, ref.at[first + i], recv_sem).wait_recv()
 
@@ -421,10 +406,10 @@
         copy.wait()
     make_turns(turn, step, turns)
 
-    gather(recv_t, rt, fst, frt)
+    gather(recv_t, rt, fst, frt, lambda i: lax.div(first + i, 8) != row)
     forward_front(recv_t, left, turns, mid, grid_f32, c_high, c_low)
     taps_spectrum(right, c_high, c_low, spectrum)
-    gather(recv_x, rx, fsx, frx)
+    gather(recv_x, rx, fsx, frx, lambda i: first + i != shard)
     forward_front(recv_x, left, turns, mid, grid_f32, c_high, c_low)
     middle(right, undo, c_high, c_low, spectrum, back_grid)
     inverse_back(turns, mid, back_grid, d_high, d_low)
@@ -484,12 +469,23 @@
         results[-1].start()
 
     def sent(i):
-        out_t(i).wait_send()
         out_x(i).wait_send()
         out_g(i).wait_send()
         out_o(i).wait_send()
 
     others(sent)
+    along_ring(lambda i: ring_copy(i, col).wait_send())
+
+    def rows_sent(block, carry):
+        for side in range(2):
+
+            @pl.when(first + side * 8 + col != shard)
+            def _():
+                row_copy(block, side).wait_send()
+
+        return carry
+
+    lax.fori_loop(0, 8, rows_sent, 0)
 
     def passed(i, carry):
         to_mate(i, recv_t, first + i, fst, frt).wait_send()
@@ -525,6 +521,7 @@
         vmem((16, 64, 128), BF16),
         vmem((16, 64, 128), BF16),
         vmem((64, 128), BF16),
+        vmem((8, 64, 128), BF16),
         vmem((32, 64, 128), BF16),
         vmem((32, 64, 128), BF16),
         vmem((16, 64, 128), BF16),
@@ -545,11 +542,12 @@
         dma((4,)),
         dma((7,)),
         dma((4,)),
+        dma((8,)),
+        dma((8,)),
         *[dma((16,)) for _ in range(12)],
         dma((4,)),
         dma((4,)),
         dma((2,)),
-        pltpu.SemaphoreType.REGULAR((17,)),
     ]
     return pl.pallas_call(
         kernel,

time: 50.5 us -> 45.9 us (0.909)
  Pallas kernels: 48.7 us -> 44 us
    pallas_call x1, Pallas kernels: 48.7 us -> 44 us  [local(): pl.pallas_call(kernel, out_shape=jax.ShapeDtypeStruct(signal.shape, BF16)...]
where the time goes in v2:
time: 45.9 us; the launch traced here: 45.7 us
  Pallas kernels  44 us (96%)
  local copies, waits for them, and re-layouts  1.67 us (4%)
    pallas_call x1, Pallas kernels, local(): pl.pallas_call(kernel, out_shape=jax.ShapeDtypeStruct(signal.shape, BF16)...  44 us
    unnamed x1, local copies, waits for them, and re-layouts  1.67 us

profile of v2, /device:TPU:1, one launch (start us, length us, event | category | flops | bytes accessed | tf_op | source)
XLA Modules:
  0.0 45.7 jit_solution(10814346167328384241)
XLA Ops:
  0.0 44.0 %hyena.1 = bf16[16,8192]{1,0:T(8,128)(2,1)} custom-call(bf16[16,8192]{1,0:T(8,128)(2,1)} %signal_in.1, bf16[1,8192]{1,0:T(2,128)(2,1)} %taps_in.1, bf16[16,8192]{1,0:T(8,128)(2,1)} %gate_in.1, f32[16]{0:T(128)} %skip_in.1, bf16[2,2,256,256]{3,2,1,0:T(8,128)(2,1)} %constant.14.clone.left_all, bf16[2,2,256,256]{3,2,1,0:T(8,128)(2,1)} %constant.15.clone.back_all, ...), custom_call_target="tpu_custom_call" | custom-call | tf_op jit(solution)/shard_map/hyena/pallas_call | solution.py:552
  44.1 1.7 %copy.13 = bf16[16,8192]{1,0:T(8,128)(2,1)} copy(bf16[16,8192]{1,0:T(8,128)(2,1)} %hyena.1) | data formatting | bytes 524288

commit v3 on v2

--- a/solution.py
+++ b/solution.py
@@ -150,7 +150,7 @@
     lax.fori_loop(0, 8, body, 0)
 
 
-def taps_spectrum(right, c_high, c_low, spectrum):
+def spectrum_of(right, c_high, c_low, spectrum):
     for m in range(4):
         rows = slice(256 * m, 256 * m + 256)
         high, low = c_high[rows, :], c_low[rows, :]
@@ -333,9 +333,29 @@
     def out_o(i):
         return peer_copy(i, send_o.at[i], recv_o.at[spot], so, ro.at[spot])
 
-    along_ring(lambda i: ring_copy(i, col).start())
+    def near(i):
+        @pl.when(i != lax.rem(col + 4, 8))
+        def _():
+            ring_copy(i, col).start()
+
+    along_ring(near)
     ring_t[col] = send_t[...]
-    others(lambda i: out_x(i).start())
+    before = lax.rem(col + 5, 8)
+    far = 8 + lax.rem(col + 4, 8)
+
+    def from_far(body):
+        def run(k, carry):
+            i = lax.rem(far + k, 16)
+
+            @pl.when(first + i != shard)
+            def _():
+                body(i)
+
+            return carry
+
+        lax.fori_loop(0, 16, run, 0)
+
+    from_far(lambda i: out_x(i).start())
 
     @pl.when(core == half)
     def _():
@@ -343,12 +363,6 @@
 
     inputs[2].wait()
     spread_out(gate, work, send_g)
-    others(lambda i: out_g(i).start())
-
-    @pl.when(core == half)
-    def _():
-        recv_g[spot] = send_g[spot]
-
     inputs[3].wait()
     for r in range(16):
         skips[core, r : r + 1, :] = jnp.full((1, 128), skip[r], F32)
@@ -374,11 +388,29 @@
 
     to_rows(col)
 
+    def ring_on(i):
+        return pltpu.make_async_remote_copy(
+            src_ref=ring_t.at[i], dst_ref=ring_t.at[i], send_sem=sr.at[col], recv_sem=rr.at[i],
+            device_id=ring(lax.rem(col + 1, 8)), device_id_type=MESH,
+        )
+
     def relay(i):
         ring_copy(i, i).wait_recv()
+
+        @pl.when(i == before)
+        def _():
+            ring_on(i).start()
+
         to_rows(i)
 
-    along_ring(relay)
+    for k in (5, 1, 7, 2, 6, 3, 4):
+        relay(lax.rem(col + k, 8))
+    others(lambda i: out_g(i).start())
+
+    @pl.when(core == half)
+    def _():
+        recv_g[spot] = send_g[spot]
+
 
     def to_mate(i, ref, slot, send_sem, recv_sem):
         return pltpu.make_async_remote_copy(
@@ -386,7 +418,7 @@
             recv_sem=recv_sem.at[i], device_id=mate, device_id_type=MESH,
         )
 
-    def gather(ref, recv_sem, fwd_send, fwd_recv, remote):
+    def hand_over(ref, recv_sem, fwd_send, fwd_recv, remote):
         def pass_on(i):
             @pl.when(remote(i))
             def _():
@@ -396,6 +428,7 @@
 
         all_peers(pass_on)
 
+    def take_over(ref, fwd_send, fwd_recv):
         def take(i, carry):
             to_mate(i, ref, other + i, fwd_send, fwd_recv).wait_recv()
             return carry
@@ -406,11 +439,13 @@
         copy.wait()
     make_turns(turn, step, turns)
 
-    gather(recv_t, rt, fst, frt, lambda i: lax.div(first + i, 8) != row)
+    hand_over(recv_x, rx, fsx, frx, lambda i: first + i != shard)
+    hand_over(recv_t, rt, fst, frt, lambda i: lax.div(first + i, 8) != row)
+    take_over(recv_x, fsx, frx)
+    forward_front(recv_x, left, turns, mid, grid_f32, c_high, c_low)
+    spectrum_of(right, c_high, c_low, spectrum)
+    take_over(recv_t, fst, frt)
     forward_front(recv_t, left, turns, mid, grid_f32, c_high, c_low)
-    taps_spectrum(right, c_high, c_low, spectrum)
-    gather(recv_x, rx, fsx, frx, lambda i: first + i != shard)
-    forward_front(recv_x, left, turns, mid, grid_f32, c_high, c_low)
     middle(right, undo, c_high, c_low, spectrum, back_grid)
     inverse_back(turns, mid, back_grid, d_high, d_low)
 
@@ -474,7 +509,14 @@
         out_o(i).wait_send()
 
     others(sent)
-    along_ring(lambda i: ring_copy(i, col).wait_send())
+
+    def ring_sent(i):
+        @pl.when(i != lax.rem(col + 4, 8))
+        def _():
+            ring_copy(i, col).wait_send()
+
+    along_ring(ring_sent)
+    ring_on(before).wait_send()
 
     def rows_sent(block, carry):
         for side in range(2):

time: 45.9 us -> 44.2 us (0.963)
  Pallas kernels: 44 us -> 42.4 us
    pallas_call x1, Pallas kernels: 44 us -> 42.4 us  [local(): pl.pallas_call(kernel, out_shape=jax.ShapeDtypeStruct(signal.shape, BF16)...]
where the time goes in v3:
time: 44.2 us; the launch traced here: 44.1 us
  Pallas kernels  42.4 us (96%)
  local copies, waits for them, and re-layouts  1.67 us (4%)
    pallas_call x1, Pallas kernels, local(): pl.pallas_call(kernel, out_shape=jax.ShapeDtypeStruct(signal.shape, BF16)...  42.4 us
    unnamed x1, local copies, waits for them, and re-layouts  1.67 us

profile of v3, /device:TPU:1, one launch (start us, length us, event | category | flops | bytes accessed | tf_op | source)
XLA Modules:
  0.0 44.1 jit_solution(6286185931614045275)
XLA Ops:
  0.0 42.4 %hyena.1 = bf16[16,8192]{1,0:T(8,128)(2,1)} custom-call(bf16[16,8192]{1,0:T(8,128)(2,1)} %signal_in.1, bf16[1,8192]{1,0:T(2,128)(2,1)} %taps_in.1, bf16[16,8192]{1,0:T(8,128)(2,1)} %gate_in.1, f32[16]{0:T(128)} %skip_in.1, bf16[2,2,256,256]{3,2,1,0:T(8,128)(2,1)} %constant.14.clone.left_all, bf16[2,2,256,256]{3,2,1,0:T(8,128)(2,1)} %constant.15.clone.back_all, ...), custom_call_target="tpu_custom_call" | custom-call | tf_op jit(solution)/shard_map/hyena/pallas_call | solution.py:594
  42.4 1.7 %copy.13 = bf16[16,8192]{1,0:T(8,128)(2,1)} copy(bf16[16,8192]{1,0:T(8,128)(2,1)} %hyena.1) | data formatting | bytes 524288

commit v4 on v3

--- a/solution.py
+++ b/solution.py
@@ -121,7 +121,7 @@
     lax.fori_loop(0, 8, body, 0)
 
 
-def forward_front(data, left, turns, mid, grid_f32, c_high, c_low):
+def first_stage(data, left, grid_f32):
     for c in range(4):
         tile = data[:, 16 * c : 16 * c + 16, :].astype(F32)
         block = jnp.concatenate(
@@ -129,65 +129,57 @@
         ).astype(BF16)
         grid_f32[:, 256 * c : 256 * c + 256] = mm(left[0], block) + mm(left[1], block)
 
-    def body(q, carry):
-        at = pl.multiple_of(q * 16, 16)
-        z = []
-        for a in range(8):
-            cols = slice(128 * a, 128 * a + 128)
-            value = (grid_f32[pl.ds(at, 16), cols], grid_f32[pl.ds(at + 128, 16), cols])
-            z.append(times(value, (turns[0, a, pl.ds(at, 16), :], turns[1, a, pl.ds(at, 16), :])))
-        z = dft8(z, -1)
-        for ka in range(8):
-            value = z[ka]
-            if ka:
-                value = times(value, (mid[0, ka : ka + 1, :], mid[1, ka : ka + 1, :]))
-            rows = pl.ds(pl.multiple_of(at + 128 * ka, 16), 16)
-            for part in range(2):
-                cols = slice(128 * part, 128 * part + 128)
-                c_high[rows, cols], c_low[rows, cols] = split(value[part])
-        return carry
-
-    lax.fori_loop(0, 8, body, 0)
-
-
-def spectrum_of(right, c_high, c_low, spectrum):
+
+def second_stage(at, turns, mid, grid_f32):
+    rows = slice(at, at + 16)
+    z = []
+    for a in range(8):
+        cols = slice(128 * a, 128 * a + 128)
+        value = (grid_f32[rows, cols], grid_f32[at + 128 : at + 144, cols])
+        z.append(times(value, (turns[0, a, rows, :], turns[1, a, rows, :])))
+    z = dft8(z, -1)
+    for ka in range(1, 8):
+        z[ka] = times(z[ka], (mid[0, ka : ka + 1, :], mid[1, ka : ka + 1, :]))
+    return split(jnp.concatenate([jnp.concatenate(v, axis=1) for v in z], axis=0))
+
+
+def transform_rows(m, right, turns, mid, grid_f32):
+    parts = [second_stage(32 * m + 16 * o, turns, mid, grid_f32) for o in range(2)]
+    high = jnp.concatenate([p[0] for p in parts], axis=0)
+    low = jnp.concatenate([p[1] for p in parts], axis=0)
+    return mm(high, right[0]) + mm(low, right[0]) + mm(high, right[1])
+
+
+def spectrum_of(data, left, right, turns, mid, grid_f32, spectrum):
+    first_stage(data, left, grid_f32)
     for m in range(4):
-        rows = slice(256 * m, 256 * m + 256)
-        high, low = c_high[rows, :], c_low[rows, :]
-        spectrum[rows, :] = mm(high, right[0]) + mm(low, right[0]) + mm(high, right[1])
-
-
-def middle(right, undo, c_high, c_low, spectrum, back_grid):
+        spectrum[256 * m : 256 * m + 256, :] = transform_rows(m, right, turns, mid, grid_f32)
+
+
+def middle(data, left, right, undo, turns, mid, grid_f32, spectrum, d_high, d_low):
+    first_stage(data, left, grid_f32)
     for m in range(4):
-        rows = slice(256 * m, 256 * m + 256)
-        high, low = c_high[rows, :], c_low[rows, :]
-        value = mm(high, right[0]) + mm(low, right[0]) + mm(high, right[1])
-        taps = spectrum[rows, :]
-        re, im = times((value[:, :128], value[:, 128:]), (taps[:, :128], taps[:, 128:]))
+        value = transform_rows(m, right, turns, mid, grid_f32)
+        known = spectrum[256 * m : 256 * m + 256, :]
+        re, im = times((value[:, :128], value[:, 128:]), (known[:, :128], known[:, 128:]))
         high, low = split(jnp.concatenate([re, im], axis=1))
-        back_grid[rows, :] = mm(high, undo[0]) + mm(low, undo[0]) + mm(high, undo[1])
-
-
-def inverse_back(turns, mid, back_grid, d_high, d_low):
-    def body(q, carry):
-        at = pl.multiple_of(q * 16, 16)
-        z = []
-        for ka in range(8):
-            rows = pl.ds(pl.multiple_of(at + 128 * ka, 16), 16)
-            value = (back_grid[rows, 0:128], back_grid[rows, 128:256])
-            if ka:
-                value = times_conj(value, (mid[0, ka : ka + 1, :], mid[1, ka : ka + 1, :]))
-            z.append(value)
-        z = dft8(z, 1)
-        for a in range(8):
-            value = times_conj(z[a], (turns[0, a, pl.ds(at, 16), :], turns[1, a, pl.ds(at, 16), :]))
-            cols = slice(128 * a, 128 * a + 128)
-            for part in range(2):
-                rows = pl.ds(pl.multiple_of(at + 128 * part, 16), 16)
-                d_high[rows, cols], d_low[rows, cols] = split(value[part])
-        return carry
-
-    lax.fori_loop(0, 8, body, 0)
+        value = mm(high, undo[0]) + mm(low, undo[0]) + mm(high, undo[1])
+        for o in range(2):
+            at = 32 * m + 16 * o
+            z = []
+            for ka in range(8):
+                rows = slice(128 * o + 16 * ka, 128 * o + 16 * ka + 16)
+                z.append((value[rows, :128], value[rows, 128:]))
+                if ka:
+                    z[ka] = times_conj(z[ka], (mid[0, ka : ka + 1, :], mid[1, ka : ka + 1, :]))
+            z = dft8(z, 1)
+            for a in range(8):
+                rows = slice(at, at + 16)
+                back = times_conj(z[a], (turns[0, a, rows, :], turns[1, a, rows, :]))
+                cols = slice(128 * a, 128 * a + 128)
+                for part in range(2):
+                    rows = slice(at + 128 * part, at + 128 * part + 16)
+                    d_high[rows, cols], d_low[rows, cols] = split(back[part])
 
 
 def inverse_columns(c, back, d_high, d_low):
@@ -219,7 +211,7 @@
     signal, taps, gate, skip, out,
     left, back, turn, step, right, undo, mid,
     work, taps_work, send_x, send_g, send_t, ring_t, recv_x, recv_t, recv_g, send_o, recv_o, skips,
-    turns, grid_f32, c_high, c_low, spectrum, back_grid, d_high, d_low, y_mine, y_send, y_recv,
+    turns, grid_f32, spectrum, d_high, d_low, y_mine, y_send, y_recv,
     input_sems, table_sems, out_sems,
     sr, rr, sx, rx, st, rt, sg, rg, so, ro, fsx, frx, fst, frt, sy, ry, skip_sems,
 ):
@@ -343,17 +335,21 @@
     before = lax.rem(col + 5, 8)
     far = 8 + lax.rem(col + 4, 8)
 
-    def from_far(body):
+    def in_order(body):
         def run(k, carry):
             i = lax.rem(far + k, 16)
-
+            body(i)
+            return carry
+
+        lax.fori_loop(0, 16, run, 0)
+
+    def from_far(body):
+        def run(i):
             @pl.when(first + i != shard)
             def _():
                 body(i)
 
-            return carry
-
-        lax.fori_loop(0, 16, run, 0)
+        in_order(run)
 
     from_far(lambda i: out_x(i).start())
 
@@ -442,12 +438,9 @@
     hand_over(recv_x, rx, fsx, frx, lambda i: first + i != shard)
     hand_over(recv_t, rt, fst, frt, lambda i: lax.div(first + i, 8) != row)
     take_over(recv_x, fsx, frx)
-    forward_front(recv_x, left, turns, mid, grid_f32, c_high, c_low)
-    spectrum_of(right, c_high, c_low, spectrum)
+    spectrum_of(recv_x, left, right, turns, mid, grid_f32, spectrum)
     take_over(recv_t, fst, frt)
-    forward_front(recv_t, left, turns, mid, grid_f32, c_high, c_low)
-    middle(right, undo, c_high, c_low, spectrum, back_grid)
-    inverse_back(turns, mid, back_grid, d_high, d_low)
+    middle(recv_t, left, right, undo, turns, mid, grid_f32, spectrum, d_high, d_low)
 
     def y_copy(c):
         return pltpu.make_async_remote_copy(
@@ -484,7 +477,7 @@
         def _():
             recv_o[spot] = send_o[i]
 
-    all_peers(send_back)
+    in_order(send_back)
 
     def place(i):
         @pl.when(first + i != shard)
@@ -572,9 +565,6 @@
         vmem((2, 16, 128), F32),
         vmem((2, 8, 128, 128), F32),
         vmem((256, 1024), F32),
-        vmem((1024, 256), BF16),
-        vmem((1024, 256), BF16),
-        vmem((1024, 256), F32),
         vmem((1024, 256), F32),
         vmem((256, 1024), BF16),
         vmem((256, 1024), BF16),

time: 44.2 us -> 42.1 us (0.952)
  Pallas kernels: 42.4 us -> 40.3 us
    pallas_call x1, Pallas kernels: 42.4 us -> 40.3 us  [local(): pl.pallas_call(kernel, out_shape=jax.ShapeDtypeStruct(signal.shape, BF16)...]
where the time goes in v4:
time: 42.1 us; the launch traced here: 42 us
  Pallas kernels  40.3 us (96%)
  local copies, waits for them, and re-layouts  1.67 us (4%)
    pallas_call x1, Pallas kernels, local(): pl.pallas_call(kernel, out_shape=jax.ShapeDtypeStruct(signal.shape, BF16)...  40.3 us
    unnamed x1, local copies, waits for them, and re-layouts  1.67 us

profile of v4, /device:TPU:1, one launch (start us, length us, event | category | flops | bytes accessed | tf_op | source)
XLA Modules:
  0.0 42.0 jit_solution(9502897953467714347)
XLA Ops:
  0.0 40.3 %hyena.1 = bf16[16,8192]{1,0:T(8,128)(2,1)} custom-call(bf16[16,8192]{1,0:T(8,128)(2,1)} %signal_in.1, bf16[1,8192]{1,0:T(2,128)(2,1)} %taps_in.1, bf16[16,8192]{1,0:T(8,128)(2,1)} %gate_in.1, f32[16]{0:T(128)} %skip_in.1, bf16[2,2,256,256]{3,2,1,0:T(8,128)(2,1)} %constant.14.clone.left_all, bf16[2,2,256,256]{3,2,1,0:T(8,128)(2,1)} %constant.15.clone.back_all, ...), custom_call_target="tpu_custom_call" | custom-call | tf_op jit(solution)/shard_map/hyena/pallas_call | solution.py:584
  40.3 1.7 %copy.13 = bf16[16,8192]{1,0:T(8,128)(2,1)} copy(bf16[16,8192]{1,0:T(8,128)(2,1)} %hyena.1) | data formatting | bytes 524288

commit v5 on v4

--- a/solution.py
+++ b/solution.py
@@ -207,12 +207,12 @@
 
 def kernel(
     signal_in, taps_in, gate_in, skip_in, left_all, back_all, turn_all, step_all, right_all, undo_all, mid_all,
-    out_all,
-    signal, taps, gate, skip, out,
+    out,
+    signal, taps, gate, skip,
     left, back, turn, step, right, undo, mid,
     work, taps_work, send_x, send_g, send_t, ring_t, recv_x, recv_t, recv_g, send_o, recv_o, skips,
     turns, grid_f32, spectrum, d_high, d_low, y_mine, y_send, y_recv,
-    input_sems, table_sems, out_sems,
+    input_sems, table_sems,
     sr, rr, sx, rx, st, rt, sg, rg, so, ro, fsx, frx, fst, frt, sy, ry, skip_sems,
 ):
     shard = lax.axis_index("ctx")
@@ -487,14 +487,9 @@
         put_row(recv_o, work, i)
 
     all_peers(place)
-    results = []
-    for piece in range(4):
-        for j in range(16 * piece, 16 * piece + 16):
-            at = (j // 8) * PITCH + (j % 8) * 16
-            out[piece, :, 128 * (j % 16) : 128 * (j % 16) + 128] = work[at : at + 16, :].astype(BF16)
-        cols = slice(2048 * piece, 2048 * piece + 2048)
-        results.append(pltpu.make_async_copy(out.at[piece], out_all.at[:, cols], out_sems.at[piece]))
-        results[-1].start()
+    for j in range(64):
+        at = (j // 8) * PITCH + (j % 8) * 16
+        out[:, 128 * j : 128 * j + 128] = work[at : at + 16, :].astype(BF16)
 
     def sent(i):
         out_x(i).wait_send()
@@ -530,8 +525,6 @@
     lax.fori_loop(0, 16, passed, 0)
     for c in range(4):
         y_copy(c).wait_send()
-    for result in results:
-        result.wait()
 
 
 def local(signal, filter_taps, gate_values, skip_weight):
@@ -543,7 +536,6 @@
         vmem((1, 8192), BF16),
         vmem((16, 8192), BF16),
         pltpu.SMEM((16,), F32),
-        vmem((4, 16, 2048), BF16),
         vmem((2, 256, 256), BF16),
         vmem((2, 256, 256), BF16),
         vmem((2, 128, 128), F32),
@@ -573,7 +565,6 @@
         vmem((4, 128, 256), F32),
         dma((4,)),
         dma((7,)),
-        dma((4,)),
         dma((8,)),
         dma((8,)),
         *[dma((16,)) for _ in range(12)],
@@ -583,9 +574,9 @@
     ]
     return pl.pallas_call(
         kernel,
-        out_shape=jax.ShapeDtypeStruct(signal.shape, BF16),
+        out_shape=vmem(signal.shape, BF16),
         in_specs=[apart] * (4 + len(held)),
-        out_specs=apart,
+        out_specs=pl.BlockSpec(memory_space=pltpu.VMEM),
         scratch_shapes=scratch,
         compiler_params=pltpu.CompilerParams(collective_id=0, has_side_effects=True),
         name="hyena",

time: 42.1 us -> 41 us (0.974)
  local copies, waits for them, and re-layouts: 1.67 us -> 0.71 us
    unnamed x1, local copies, waits for them, and re-layouts: 1.67 us -> 0.71 us
where the time goes in v5:
time: 41 us; the launch traced here: 40.9 us
  Pallas kernels  40.1 us (98%)
  local copies, waits for them, and re-layouts  0.71 us (2%)
    pallas_call x1, Pallas kernels, local(): pl.pallas_call(kernel, out_shape=vmem(signal.shape, BF16), in_specs=[apar...  40.1 us

profile of v5, /device:TPU:1, one launch (start us, length us, event | category | flops | bytes accessed | tf_op | source)
XLA Modules:
  0.0 40.9 jit_solution(3582575880528735494)
XLA Ops:
  0.0 40.1 %hyena.1 = bf16[16,8192]{1,0:T(8,128)(2,1)S(1)} custom-call(bf16[16,8192]{1,0:T(8,128)(2,1)} %signal_in.1, bf16[1,8192]{1,0:T(2,128)(2,1)} %taps_in.1, bf16[16,8192]{1,0:T(8,128)(2,1)} %gate_in.1, f32[16]{0:T(128)} %skip_in.1, bf16[2,2,256,256]{3,2,1,0:T(8,128)(2,1)} %constant.14.clone.left_all, bf16[2,2,256,256]{3,2,1,0:T(8,128)(2,1)} %constant.15.clone.back_all, ...), custom_call_target="tpu_custom_call" | custom-call | tf_op jit(solution)/shard_map/hyena/pallas_call | solution.py:575
  40.2 0.7 %copy.13 = bf16[16,8192]{1,0:T(8,128)(2,1)} copy(bf16[16,8192]{1,0:T(8,128)(2,1)S(1)} %hyena.1) | data formatting | bytes 524288

commit v6 on v5

--- a/solution.py
+++ b/solution.py
@@ -182,10 +182,10 @@
                     d_high[rows, cols], d_low[rows, cols] = split(back[part])
 
 
-def inverse_columns(c, back, d_high, d_low):
+def inverse_columns(c, rows, back, d_high, d_low):
     cols = slice(256 * c, 256 * c + 256)
     high, low = d_high[:, cols], d_low[:, cols]
-    return mm(back[0], high) + mm(back[0], low) + mm(back[1], high)
+    return mm(back[0, rows, :], high) + mm(back[0, rows, :], low) + mm(back[1, rows, :], high)
 
 
 def spread_out(rows_ref, work, send):
@@ -228,12 +228,12 @@
     def peer(i):
         return {"ctx": first + i, "core": half}
 
-    def all_peers(body):
+    def all_peers(body, unroll=1):
         def run(k, carry):
             body(lax.rem(spot + k, 16))
             return carry
 
-        lax.fori_loop(0, 16, run, 0)
+        lax.fori_loop(0, 16, run, 0, unroll=unroll)
 
     barrier = pltpu.get_barrier_semaphore()
 
@@ -335,13 +335,13 @@
     before = lax.rem(col + 5, 8)
     far = 8 + lax.rem(col + 4, 8)
 
-    def in_order(body):
+    def in_order(body, unroll=1):
         def run(k, carry):
             i = lax.rem(far + k, 16)
             body(i)
             return carry
 
-        lax.fori_loop(0, 16, run, 0)
+        lax.fori_loop(0, 16, run, 0, unroll=unroll)
 
     def from_far(body):
         def run(i):
@@ -422,14 +422,11 @@
 
             to_mate(i, ref, first + i, fwd_send, fwd_recv).start()
 
-        all_peers(pass_on)
+        all_peers(pass_on, 4)
 
     def take_over(ref, fwd_send, fwd_recv):
-        def take(i, carry):
+        for i in range(16):
             to_mate(i, ref, other + i, fwd_send, fwd_recv).wait_recv()
-            return carry
-
-        lax.fori_loop(0, 16, take, 0)
 
     for copy in copies:
         copy.wait()
@@ -449,10 +446,10 @@
         )
 
     for c in range(4):
-        value = inverse_columns(c, back, d_high, d_low)
-        y_send[c] = value[128:, :]
-        y_mine[c] = value[:128, :]
+        y_send[c] = inverse_columns(c, slice(128, 256), back, d_high, d_low)
         y_copy(c).start()
+    for c in range(4):
+        y_mine[c] = inverse_columns(c, slice(0, 128), back, d_high, d_low)
     skip_copy.wait()
     weight = skips[half, pl.ds(spot, 1), :]
     others(lambda i: incoming(i, recv_g.at[i], rg).wait_recv())
@@ -477,19 +474,7 @@
         def _():
             recv_o[spot] = send_o[i]
 
-    in_order(send_back)
-
-    def place(i):
-        @pl.when(first + i != shard)
-        def _():
-            incoming(i, recv_o.at[i], ro).wait_recv()
-
-        put_row(recv_o, work, i)
-
-    all_peers(place)
-    for j in range(64):
-        at = (j // 8) * PITCH + (j % 8) * 16
-        out[:, 128 * j : 128 * j + 128] = work[at : at + 16, :].astype(BF16)
+    in_order(send_back, 4)
 
     def sent(i):
         out_x(i).wait_send()
@@ -525,6 +510,18 @@
     lax.fori_loop(0, 16, passed, 0)
     for c in range(4):
         y_copy(c).wait_send()
+
+    def place(i):
+        @pl.when(first + i != shard)
+        def _():
+            incoming(i, recv_o.at[i], ro).wait_recv()
+
+        put_row(recv_o, work, i)
+
+    all_peers(place, 4)
+    for j in range(64):
+        at = (j // 8) * PITCH + (j % 8) * 16
+        out[:, 128 * j : 128 * j + 128] = work[at : at + 16, :].astype(BF16)
 
 
 def local(signal, filter_taps, gate_values, skip_weight):

time: 41 us -> 39.8 us (0.971)
  Pallas kernels: 40.1 us -> 39 us
    pallas_call x1, Pallas kernels: 40.1 us -> 39 us  [local(): pl.pallas_call(kernel, out_shape=vmem(signal.shape, BF16), in_specs=[apar...]
where the time goes in v6:
time: 39.8 us; the launch traced here: 39.7 us
  Pallas kernels  39 us (98%)
  local copies, waits for them, and re-layouts  0.71 us (2%)
    pallas_call x1, Pallas kernels, local(): pl.pallas_call(kernel, out_shape=vmem(signal.shape, BF16), in_specs=[apar...  39 us

profile of v6, /device:TPU:1, one launch (start us, length us, event | category | flops | bytes accessed | tf_op | source)
XLA Modules:
  0.0 39.7 jit_solution(2033993030831196252)
XLA Ops:
  0.0 39.0 %hyena.1 = bf16[16,8192]{1,0:T(8,128)(2,1)S(1)} custom-call(bf16[16,8192]{1,0:T(8,128)(2,1)} %signal_in.1, bf16[1,8192]{1,0:T(2,128)(2,1)} %taps_in.1, bf16[16,8192]{1,0:T(8,128)(2,1)} %gate_in.1, f32[16]{0:T(128)} %skip_in.1, bf16[2,2,256,256]{3,2,1,0:T(8,128)(2,1)} %constant.14.clone.left_all, bf16[2,2,256,256]{3,2,1,0:T(8,128)(2,1)} %constant.15.clone.back_all, ...), custom_call_target="tpu_custom_call" | custom-call | tf_op jit(solution)/shard_map/hyena/pallas_call | solution.py:572
  39.0 0.7 %copy.13 = bf16[16,8192]{1,0:T(8,128)(2,1)} copy(bf16[16,8192]{1,0:T(8,128)(2,1)S(1)} %hyena.1) | data formatting | bytes 524288

commit v7 on v6

--- a/solution.py
+++ b/solution.py
@@ -228,7 +228,7 @@
     def peer(i):
         return {"ctx": first + i, "core": half}
 
-    def all_peers(body, unroll=1):
+    def all_peers(body, unroll=4):
         def run(k, carry):
             body(lax.rem(spot + k, 16))
             return carry
@@ -253,7 +253,7 @@
             body(lax.rem(col + k, 8))
             return carry
 
-        lax.fori_loop(1, 8, run, 0)
+        lax.fori_loop(1, 8, run, 0, unroll=7)
 
     def hello(device):
         pl.semaphore_signal(barrier, inc=1, device_id=device, device_id_type=MESH)
@@ -335,7 +335,7 @@
     before = lax.rem(col + 5, 8)
     far = 8 + lax.rem(col + 4, 8)
 
-    def in_order(body, unroll=1):
+    def in_order(body, unroll=4):
         def run(k, carry):
             i = lax.rem(far + k, 16)
             body(i)

time: 39.8 us -> 40.3 us (1.013)
  Pallas kernels: 39 us -> 39.5 us
    pallas_call x1, Pallas kernels: 39 us -> 39.5 us  [local(): pl.pallas_call(kernel, out_shape=vmem(signal.shape, BF16), in_specs=[apar...]
where the time goes in v7:
time: 40.3 us
  Pallas kernels  39.5 us (98%)
  local copies, waits for them, and re-layouts  0.71 us (2%)
    pallas_call x1, Pallas kernels, local(): pl.pallas_call(kernel, out_shape=vmem(signal.shape, BF16), in_specs=[apar...  39.5 us

profile of v7, /device:TPU:1, one launch (start us, length us, event | category | flops | bytes accessed | tf_op | source)
XLA Modules:
  0.0 40.3 jit_solution(17293628358056310667)
XLA Ops:
  0.0 39.5 %hyena.1 = bf16[16,8192]{1,0:T(8,128)(2,1)S(1)} custom-call(bf16[16,8192]{1,0:T(8,128)(2,1)} %signal_in.1, bf16[1,8192]{1,0:T(2,128)(2,1)} %taps_in.1, bf16[16,8192]{1,0:T(8,128)(2,1)} %gate_in.1, f32[16]{0:T(128)} %skip_in.1, bf16[2,2,256,256]{3,2,1,0:T(8,128)(2,1)} %constant.14.clone.left_all, bf16[2,2,256,256]{3,2,1,0:T(8,128)(2,1)} %constant.15.clone.back_all, ...), custom_call_target="tpu_custom_call" | custom-call | tf_op jit(solution)/shard_map/hyena/pallas_call | solution.py:572
  39.5 0.7 %copy.13 = bf16[16,8192]{1,0:T(8,128)(2,1)} copy(bf16[16,8192]{1,0:T(8,128)(2,1)S(1)} %hyena.1) | data formatting | bytes 524288
